TPU v7x, 32 devices: a 4x4x1 block of a 4x4x8 slice. The times are simulated.
32 devices in a mesh: dp: 1 (over z), tp: 32 (over y, x, core).
Axes of the slice: x: 4, y: 4, z: 1, core: 2. Of those that a mesh axis runs over, the one named last changes fastest.
The devices are a block of a 4x4x8 slice.
Arguments:
- tokens: bfloat16 [1, 2048, 4096], P('dp', 'tp')
- doc_ids: int32 [1, 2048], P('dp', 'tp')
- norm1_gain: float32 [2, 4096], replicated
- norm1_shift: float32 [2, 4096], replicated
- qkv_weight: bfloat16 [2, 4096, 3, 32, 128], P(None, None, None, 'tp')
- out_weight: bfloat16 [2, 32, 128, 4096], P(None, 'tp')
- out_bias: float32 [2, 4096], replicated
- norm2_gain: float32 [2, 4096], replicated
- norm2_shift: float32 [2, 4096], replicated
- up_weight: bfloat16 [2, 4096, 16384], P(None, None, 'tp')
- up_bias: float32 [2, 16384], P(None, 'tp')
- down_weight: bfloat16 [2, 16384, 4096], P(None, 'tp')
- down_bias: float32 [2, 4096], replicated
Outputs:
- output: bfloat16 [1, 2048, 4096], P('dp', 'tp')
All inputs are finite; a program needn't handle non-finite values.
Results may differ from a plain program's by a relative error of at most 0.0120228.
Values are sent between devices in bfloat16 or wider.
A program may use at most 768 MiB of HBM per device.

v0:
```python
import jax
import jax.numpy as jnp
from jax import lax
from jax.sharding import PartitionSpec as P, NamedSharding

QUERY_ROWS = 512


def layer_norm(residual, gain_vec, shift_vec):
    mean_val = jnp.mean(residual, axis=-1, keepdims=True)
    centered = residual - mean_val
    variance = jnp.mean(centered * centered, axis=-1, keepdims=True)
    return (centered * lax.rsqrt(variance + 1e-5) * gain_vec + shift_vec).astype(jnp.bfloat16)


def doc_causal_attention(queries, keys_in, values_in, all_ids):
    seq_len = queries.shape[2]
    score_scale = queries.shape[3] ** -0.5
    block_rows = min(QUERY_ROWS, seq_len)
    pieces = []
    for start_row in range(0, seq_len, block_rows):
        stop_row = start_row + block_rows
        scores = jnp.einsum("bhqe,bhke->bhqk", queries[:, :, start_row:stop_row], keys_in[:, :, :stop_row], preferred_element_type=jnp.float32) * score_scale
        query_pos = start_row + jnp.arange(block_rows)
        key_pos = jnp.arange(stop_row)
        allowed = (key_pos[None, None, :] <= query_pos[None, :, None]) & (all_ids[:, start_row:stop_row, None] == all_ids[:, None, :stop_row])
        scores = jnp.where(allowed[:, None], scores, -1e30)
        probs_blk = jax.nn.softmax(scores, axis=-1).astype(jnp.bfloat16)
        pieces.append(jnp.einsum("bhqk,bhke->bqhe", probs_blk, values_in[:, :, :stop_row], preferred_element_type=jnp.float32).astype(jnp.bfloat16))
    return jnp.concatenate(pieces, axis=1)


def scatter_sum(partial_rows, groups):
    n_batch, seq_len, model_dim = partial_rows.shape
    split_rows = partial_rows.reshape(n_batch, groups, seq_len // groups, model_dim)
    received = lax.all_to_all(split_rows, "tp", 1, 1, tiled=True)
    return jnp.sum(received, axis=1, dtype=jnp.float32)


def solution(mesh):
    groups = mesh.shape["tp"]
    row_spec = P("dp", "tp", None)
    vec_spec = P(None, None)
    in_specs = (row_spec, P("dp", "tp"), vec_spec, vec_spec, P(None, None, None, "tp", None), P(None, "tp", None, None), vec_spec, vec_spec, vec_spec, P(None, None, "tp"), P(None, "tp"), P(None, "tp", None), vec_spec)

    def device_fn(tokens, doc_ids, norm1_gain, norm1_shift, qkv_weight, out_weight, out_bias, norm2_gain, norm2_shift, up_weight, up_bias, down_weight, down_bias):
        all_ids = lax.all_gather(doc_ids, "tp", axis=1, tiled=True)
        residual = tokens.astype(jnp.float32)
        for layer_idx in range(norm1_gain.shape[0]):
            normed = layer_norm(residual, norm1_gain[layer_idx], norm1_shift[layer_idx])
            full_rows = lax.all_gather(normed, "tp", axis=1, tiled=True)
            qkv_heads = jnp.einsum("bsd,dthe->tbhse", full_rows, qkv_weight[layer_idx], preferred_element_type=jnp.float32).astype(jnp.bfloat16)
            attn_out = doc_causal_attention(qkv_heads[0], qkv_heads[1], qkv_heads[2], all_ids)
            attn_part = jnp.einsum("bshe,hed->bsd", attn_out, out_weight[layer_idx], preferred_element_type=jnp.float32).astype(jnp.bfloat16)
            residual = residual + (scatter_sum(attn_part, groups) + out_bias[layer_idx])
            normed2 = layer_norm(residual, norm2_gain[layer_idx], norm2_shift[layer_idx])
            full_rows2 = lax.all_gather(normed2, "tp", axis=1, tiled=True)
            pre_act = jnp.einsum("bsd,df->bsf", full_rows2, up_weight[layer_idx], preferred_element_type=jnp.float32) + up_bias[layer_idx]
            hidden = jax.nn.gelu(pre_act, approximate=True).astype(jnp.bfloat16)
            mlp_part = jnp.einsum("bsf,fd->bsd", hidden, down_weight[layer_idx], preferred_element_type=jnp.float32).astype(jnp.bfloat16)
            residual = residual + (scatter_sum(mlp_part, groups) + down_bias[layer_idx])
        return residual.astype(jnp.bfloat16)

    return jax.shard_map(device_fn, mesh=mesh, in_specs=in_specs, out_specs=row_spec, check_vma=False)
```

profile of v0, /device:TPU:97, one launch (start us, length us, event | category | flops | bytes accessed | tf_op | source)
XLA Modules:
  0.0 1301.8 jit_solution(14009795801643836763)
XLA Ops:
  6.6 0.9 fusion.154
  7.4 0.9 fusion.155
  8.3 1.2 convert_reduce_fusion.4
  9.5 1.3 fusion.101
  10.9 2.1 fusion.104
  13.0 0.8 bitcast_dynamic-update-slice_fusion
  13.8 51.2 %all-reduce = s32[2048]{0:T(1024)S(1)} all-reduce(s32[2048]{0:T(1024)S(1)} %bitcast_dynamic-update-slice_fusion), channel_id=1, replica_groups=mesh['dp'=1,'tp'=32] {'tp'}, use_global_device_ids=true, to_apply=%add | all-reduce | flops 2048 | bytes 16384
  65.1 20.5 %all-gather.5.cloned.1.call-done = bf16[1,2048,4096]{2,1,0:T(8,128)(2,1)} async-done(((bf16[1,64,4096]{2,1,0:T(8,128)(2,1)}), bf16[1,2048,4096]{2,1,0:T(8,128)(2,1)}) %all-gather.5.cloned.1.call-update) | async-done | bytes 16777232 | tf_op jit(solution)/shard_map/all_gather | solution.py:51
  85.6 13.3 %fusion.65 = bf16[3,1,1,2048,128]{4,3,0,1,2:T(8,128)(2,1)S(1)} fusion(bf16[2,4096,3,1,128]{4,1,2,3,0:T(8,128)(2,1)} %bitcast.335, bf16[1,2048,4096]{2,1,0:T(8,128)(2,1)} %all-gather.5.cloned.1.call-done), kind=kOutput, calls=%fused_computation.69 | convolution fusion | flops 6443237376 | bytes 21495808 | tf_op jit(solution)/shard_map/bsd,dthe->tbhse/dot_general | solution.py:52
  98.9 0.1 slice_bitcast_fusion.17
  99.0 0.8 fusion.161
  99.8 0.5 fusion.81
  100.3 0.7 fusion.97
  101.0 1.0 fusion.160
  102.0 0.6 fusion.60
  102.6 0.9 fusion.99
  103.5 0.4 fusion.162
  103.9 0.2 fusion.114
  104.1 0.3 fusion.93
  104.4 1.3 fusion.159
  105.7 0.7 fusion.33
  106.5 1.1 fusion.95
  107.6 0.5 copy-done.1
  108.1 8.2 convolution_convert_fusion.3
  116.3 4.2 all-to-all-start
  120.7 204.7 %all-to-all-done = bf16[1,32,64,4096]{3,2,0,1:T(8,128)(2,1)} async-done(((bf16[1,32,64,4096]{3,2,0,1:T(8,128)(2,1)}), bf16[1,32,64,4096]{3,2,0,1:T(8,128)(2,1)}, u32[]{:S(2)}, u32[]{:S(2)}) %all-to-all-start) | async-done | bytes 16777248 | tf_op jit(solution)/shard_map/all_to_all | solution.py:36
  325.4 6.7 convert_reduce_fusion.3
  332.2 0.2 fusion.146
  332.4 0.3 multiply_reduce_fusion.2
  332.8 1.1 add_convert_fusion.2
  333.9 85.7 %all-gather.7.cloned.1.call-done = bf16[1,2048,4096]{2,1,0:T(8,128)(2,1)} async-done(((bf16[1,64,4096]{2,1,0:T(8,128)(2,1)}), bf16[1,2048,4096]{2,1,0:T(8,128)(2,1)}) %all-gather.7.cloned.1.call-update) | async-done | bytes 16777232 | tf_op jit(solution)/shard_map/all_gather | solution.py:57
  419.6 26.3 %convolution_convert_fusion.2 = bf16[2048,4096]{1,0:T(8,128)(2,1)} fusion(bf16[2,512,4096]{2,1,0:T(8,128)(2,1)} %param.24, bf16[2,4096,512]{2,1,0:T(8,128)(2,1)} %param.22, bf16[1,2048,4096]{2,1,0:T(8,128)(2,1)} %all-gather.7.cloned.1.call-done, f32[512]{0:T(512)S(1)} %bitcast.326), kind=kOutput, calls=%fused_computation.14 | convolution fusion | flops 17198743552 | bytes 41945088 | tf_op jit(solution)/shard_map/bsf,fd->bsd/dot_general | solution.py:60
  445.9 4.3 all-to-all-start.1
  450.3 203.5 %all-to-all-done.1 = bf16[1,32,64,4096]{3,2,0,1:T(8,128)(2,1)} async-done(((bf16[1,32,64,4096]{3,2,0,1:T(8,128)(2,1)}), bf16[1,32,64,4096]{3,2,0,1:T(8,128)(2,1)}, u32[]{:S(2)}, u32[]{:S(2)}) %all-to-all-start.1) | async-done | bytes 16777248 | tf_op jit(solution)/shard_map/all_to_all | solution.py:36
  653.9 6.8 convert_reduce_fusion.2
  660.6 0.3 fusion.149
  661.0 0.3 multiply_reduce_fusion.1
  661.3 1.0 add_convert_fusion.1
  662.5 86.9 %all-gather.9.cloned.1.call-done = bf16[1,2048,4096]{2,1,0:T(8,128)(2,1)} async-done(((bf16[1,64,4096]{2,1,0:T(8,128)(2,1)}), bf16[1,2048,4096]{2,1,0:T(8,128)(2,1)}) %all-gather.9.cloned.1.call-update) | async-done | bytes 16777232 | tf_op jit(solution)/shard_map/all_gather | solution.py:51
  749.3 13.5 %fusion.62 = bf16[3,1,1,2048,128]{4,3,0,1,2:T(8,128)(2,1)S(1)} fusion(bf16[2,4096,3,1,128]{4,1,2,3,0:T(8,128)(2,1)} %bitcast.336, bf16[1,2048,4096]{2,1,0:T(8,128)(2,1)} %all-gather.9.cloned.1.call-done), kind=kOutput, calls=%fused_computation.68 | convolution fusion | flops 6443237376 | bytes 21495808 | tf_op jit(solution)/shard_map/bsd,dthe->tbhse/dot_general | solution.py:52
  762.8 0.1 slice_bitcast_fusion.15
  762.9 0.4 fusion.166
  763.3 0.8 fusion.165
  764.0 1.0 fusion.164
  765.1 1.3 fusion.163
  766.4 0.2 fusion.115
  766.6 0.3 fusion.94
  767.0 0.5 fusion.82
  767.5 0.7 fusion.98
  768.2 0.6 fusion.61
  768.7 0.9 fusion.100
  769.7 0.7 fusion.34
  770.4 1.1 fusion.96
  771.5 9.6 convolution_convert_fusion.1
  781.2 204.2 %all_to_all.20 = bf16[1,32,64,4096]{3,2,0,1:T(8,128)(2,1)S(1)} all-to-all(bf16[1,32,64,4096]{3,2,0,1:T(8,128)(2,1)} %bitcast.302), channel_id=1, replica_groups=mesh['dp'=1,'tp'=32] {'tp'}, dimensions={1} | all-to-all | bytes 33554432 | tf_op jit(solution)/shard_map/all_to_all | solution.py:36
  985.4 2.4 convert_reduce_fusion.1
  987.8 0.3 fusion.147
  988.1 0.3 multiply_reduce_fusion
  988.4 1.0 add_convert_fusion
  989.5 71.5 %all-gather.11.cloned.1.call-done = bf16[1,2048,4096]{2,1,0:T(8,128)(2,1)} async-done(((bf16[1,64,4096]{2,1,0:T(8,128)(2,1)}), bf16[1,2048,4096]{2,1,0:T(8,128)(2,1)}) %all-gather.11.cloned.1.call-update) | async-done | bytes 16777232 | tf_op jit(solution)/shard_map/all_gather | solution.py:57
  1060.9 26.3 %convolution_convert_fusion = bf16[2048,4096]{1,0:T(8,128)(2,1)} fusion(bf16[2,512,4096]{2,1,0:T(8,128)(2,1)} %param.24, bf16[2,4096,512]{2,1,0:T(8,128)(2,1)} %param.22, bf16[1,2048,4096]{2,1,0:T(8,128)(2,1)} %all-gather.11.cloned.1.call-done, f32[512]{0:T(512)S(1)} %bitcast.325), kind=kOutput, calls=%fused_computation.12 | convolution fusion | flops 17198743552 | bytes 41945088 | tf_op jit(solution)/shard_map/bsf,fd->bsd/dot_general | solution.py:60
  1087.2 204.2 %all_to_all.21 = bf16[1,32,64,4096]{3,2,0,1:T(8,128)(2,1)S(1)} all-to-all(bf16[1,32,64,4096]{3,2,0,1:T(8,128)(2,1)} %bitcast.304), channel_id=1, replica_groups=mesh['dp'=1,'tp'=32] {'tp'}, dimensions={1} | all-to-all | bytes 33554432 | tf_op jit(solution)/shard_map/all_to_all | solution.py:36
  1291.4 2.4 convert_reduce_fusion
  1293.9 0.9 fusion.106
  (41 shorter events, 0.6 us)
Async XLA Ops:
  6.5 79.0 %all-gather.5.cloned.1.call-start = ((), (), s32[]{:S(2)}) async-start(), calls=%async_computation.4 | async-start | bytes 17301504 | tf_op jit(solution)/shard_map/all_gather | solution.py:51
  106.5 1.6 copy-start.1
  116.3 4.3 copy-start.2
  116.3 4.3 copy-start.3
  116.3 4.4 copy-start.4
  116.3 209.1 %all-to-all-start = ((bf16[1,32,64,4096]{3,2,0,1:T(8,128)(2,1)}), bf16[1,32,64,4096]{3,2,0,1:T(8,128)(2,1)}, u32[]{:S(2)}, u32[]{:S(2)}) async-start(bf16[1,32,64,4096]{3,2,0,1:T(8,128)(2,1)} %bitcast.301), calls=%async_computation | async-start | bytes 33554432 | tf_op jit(solution)/shard_map/all_to_all | solution.py:36
  120.5 299.1 %all-gather.7.cloned.1.call-start = ((), (), s32[]{:S(2)}) async-start(), calls=%async_computation.5 | async-start | bytes 17301504 | tf_op jit(solution)/shard_map/all_gather | solution.py:57
  120.7 211.4 %copy-start = (bf16[1,64,4096]{2,1,0:T(8,128)(2,1)S(1)}, bf16[1,64,4096]{2,1,0:T(8,128)(2,1)}, u32[]{:S(2)}) copy-start(bf16[1,64,4096]{2,1,0:T(8,128)(2,1)} %param.13) | copy-start | bytes 1572868
  332.1 1.8 copy-start.6
  445.9 4.4 copy-start.5
  445.9 208.0 %all-to-all-start.1 = ((bf16[1,32,64,4096]{3,2,0,1:T(8,128)(2,1)}), bf16[1,32,64,4096]{3,2,0,1:T(8,128)(2,1)}, u32[]{:S(2)}, u32[]{:S(2)}) async-start(bf16[1,32,64,4096]{3,2,0,1:T(8,128)(2,1)} %bitcast.303), calls=%async_computation.1 | async-start | bytes 33554432 | tf_op jit(solution)/shard_map/all_to_all | solution.py:36
  450.2 299.1 %all-gather.9.cloned.1.call-start = ((), (), s32[]{:S(2)}) async-start(), calls=%async_computation.6 | async-start | bytes 17301504 | tf_op jit(solution)/shard_map/all_gather | solution.py:51
  662.4 398.5 %all-gather.11.cloned.1.call-start = ((), (), s32[]{:S(2)}) async-start(), calls=%async_computation.7 | async-start | bytes 17301504 | tf_op jit(solution)/shard_map/all_gather | solution.py:57
Sparse Core Ops, SparseCore 0:
  13.2 72.4 all-gather.4
  334.0 85.5 all-gather.6
  662.5 86.7 all-gather.8
  989.6 71.2 all-gather.10
where the time goes:
time: 1320 us; the launch traced here: 1300 us
  waiting for transfers between devices  673 us (51%)
  blocking collectives  460 us (35%)
  matrix products  110 us (8%)
  other arithmetic  32.9 us (2%)
  between operations  13.9 us (1%)
    all_to_all x2, blocking collectives, scatter_sum(): received = lax.all_to_all(split_rows, 'tp', 1, 1, tiled=True)  408 us
    all_to_all x2, waiting for transfers between devices, scatter_sum(): received = lax.all_to_all(split_rows, 'tp', 1, 1, tiled=True)  408 us
    all_gather x2, waiting for transfers between devices, device_fn(): full_rows2 = lax.all_gather(normed2, 'tp', axis=1, tiled=True)  157 us
    all_gather x2, waiting for transfers between devices, device_fn(): full_rows = lax.all_gather(normed, 'tp', axis=1, tiled=True)  107 us
    dot_general x2, matrix products, device_fn(): jnp.einsum('bsf,fd->bsd', hidden, down_weight[layer_idx], preferred_eleme...  52.6 us
    unnamed x1, blocking collectives  51.2 us
    dot_general x2, matrix products, device_fn(): jnp.einsum('bsd,dthe->tbhse', full_rows, qkv_weight[layer_idx], preferred...  26.7 us
  transfers between devices with their start and end apart: 6, of which 6 were waited for; matrix products, arithmetic and copies ran while one was open for 0% of the time, Pallas kernels for 0%

commit v1 on v0

v1 whole, which is shorter than its diff:
```python
import functools
import math

import jax
import jax.numpy as jnp
from jax import lax
from jax.experimental import pallas as pl
from jax.experimental.pallas import tpu as pltpu
from jax.sharding import PartitionSpec as P

QUERY_ROWS = 512
COLS = 512
MESH = pl.DeviceIdType.MESH
VMEM_LIMIT = 66 * 1000 * 1000

FAR_FIRST = (2, 1, -1, 0)


class Place:
    def __init__(self, side):
        self.side = side
        self.me = lax.axis_index("tp")
        self.core = self.me % 2
        chip = self.me // 2
        self.x = chip % side
        self.y = chip // side
        self.partner = chip * 2 + 1 - self.core
        self.first = {1: self.dev(1, 0), -1: self.dev(-1, 0)}
        self.second = {1: self.dev(0, 1), -1: self.dev(0, -1)}

    def dev(self, i, j, core=None):
        core = self.core if core is None else core
        dx = i * (1 - core) + j * core
        dy = j * (1 - core) + i * core
        return (((self.y + dy + self.side) % self.side) * self.side + (self.x + dx + self.side) % self.side) * 2 + core

    def barrier(self):
        sem = pltpu.get_barrier_semaphore()
        others = [self.first[1], self.first[-1], self.second[1], self.second[-1], self.partner]
        for other in others:
            pl.semaphore_signal(sem, inc=1, device_id={"tp": other}, device_id_type=MESH)
        pl.semaphore_wait(sem, len(others))


def by_cols(width, fn):
    step = min(COLS, width)

    def body(n, carry):
        fn(pl.ds(pl.multiple_of(n * step, step), step))
        return carry

    lax.fori_loop(0, width // step, body, 0)


def scatter_kernel(side, layer, act_ref, w_hbm, res_ref, bias_ref, out_ref, w_ref, own, snd, prt, stg, mid, fin, stg2, mid2, fin2, w_sem, pair_send, pair_recv, send_sem, recv_sem):
    load_w = pltpu.make_async_copy(w_hbm.at[layer, 0] if len(w_hbm.shape) == 4 else w_hbm.at[layer], w_ref, w_sem)
    load_w.start()
    place = Place(side)
    rows, width = res_ref.shape
    half = rows // 2
    place.barrier()
    load_w.wait()

    def remote(src, dst, slot, device):
        return pltpu.make_async_remote_copy(src_ref=src, dst_ref=dst, send_sem=send_sem.at[slot], recv_sem=recv_sem.at[slot], device_id={"tp": device}, device_id_type=MESH)

    def pair_copy(g, jj):
        return pltpu.make_async_remote_copy(src_ref=snd.at[g % 2, jj], dst_ref=prt.at[g, jj], send_sem=pair_send.at[g, jj], recv_sem=pair_recv.at[g, jj], device_id={"tp": place.partner}, device_id_type=MESH)

    def product(core, g, dst):
        starts = [pl.multiple_of(place.dev(FAR_FIRST[g], j, core) * rows, rows) for j in FAR_FIRST]

        def piece(cols):
            lhs = jnp.concatenate([act_ref[pl.ds(s, rows), :] for s in starts], axis=0)
            part = jnp.dot(lhs, w_ref[:, cols], preferred_element_type=jnp.float32).astype(jnp.bfloat16)
            for jj in range(side):
                dst[jj, :, cols] = part[jj * rows:(jj + 1) * rows]

        by_cols(width, piece)

    def pair_sum(g, jj, h, cols):
        at = pl.ds(h * half, half)
        return own[g, jj, at, cols].astype(jnp.float32) + prt[g, jj, at, cols].astype(jnp.float32)

    far, plus, minus, here = range(side)
    sent = []

    def send(src, dst, slot, device):
        copy = remote(src, dst, slot, device)
        copy.start()
        sent.append(copy)

    def arrived(dst, slot):
        remote(dst, dst, slot, place.me).wait_recv()

    def open_group(g):
        for jj in range(side):
            if g >= 2:
                pair_copy(g - 2, jj).wait_send()
        product(1 - place.core, g, snd.at[g % 2])
        for jj in range(side):
            pair_copy(g, jj).start()
        product(place.core, g, own.at[g])
        for jj in range(side):
            pair_copy(g, jj).wait_recv()
        for k, (jj, h) in enumerate(((far, 0), (far, 1), (plus, 1), (minus, 0))):
            def stage(cols, k=k, jj=jj, h=h):
                stg[g, k, :, cols] = pair_sum(g, jj, h, cols)
            by_cols(width, stage)
            dst = mid.at[g, k] if k < 2 else fin.at[g, k]
            slot = 6 * g + (4 + k if k < 2 else k)
            send(stg.at[g, k], dst, slot, place.second[1 if k % 2 == 0 else -1])

    def relay(g):
        for k, (jj, h) in enumerate(((plus, 0), (minus, 1))):
            arrived(mid.at[g, k], 6 * g + 4 + k)
            def add(cols, k=k, jj=jj, h=h):
                mid[g, k, :, cols] += pair_sum(g, jj, h, cols)
            by_cols(width, add)
            send(mid.at[g, k], fin.at[g, k], 6 * g + k, place.second[1 if k == 0 else -1])

    base = 6 * side

    def close_group(g):
        for k in range(4):
            arrived(fin.at[g, k], 6 * g + k)

        def total(h, cols):
            return pair_sum(g, here, h, cols) + fin[g, 0 if h == 0 else 1, :, cols] + fin[g, 3 if h == 0 else 2, :, cols]

        def keep(k, h):
            def fn(cols):
                stg2[k, :, cols] = total(h, cols)
            by_cols(width, fn)

        def join(k):
            arrived(mid2.at[k], base + 4 + k)
            def fn(cols):
                mid2[k, :, cols] += total(k, cols)
            by_cols(width, fn)
            send(mid2.at[k], fin2.at[k], base + k, place.first[1 if k == 0 else -1])

        if g == far:
            keep(0, 0)
            send(stg2.at[0], mid2.at[0], base + 4, place.first[1])
            keep(1, 1)
            send(stg2.at[1], mid2.at[1], base + 5, place.first[-1])
        elif g == plus:
            keep(2, 1)
            send(stg2.at[2], fin2.at[2], base + 2, place.first[1])
            join(0)
        elif g == minus:
            keep(3, 0)
            send(stg2.at[3], fin2.at[3], base + 3, place.first[-1])
            join(1)
        else:
            for k in range(4):
                arrived(fin2.at[k], base + k)
            for h in range(2):
                def fn(cols, h=h):
                    at = pl.ds(h * half, half)
                    summed = total(h, cols) + fin2[0 if h == 0 else 1, :, cols] + fin2[3 if h == 0 else 2, :, cols]
                    out_ref[at, cols] = res_ref[at, cols] + (summed + bias_ref[layer:layer + 1, cols])
                by_cols(width, fn)

    open_group(0)
    open_group(1)
    relay(0)
    open_group(2)
    relay(1)
    close_group(0)
    open_group(3)
    relay(2)
    close_group(1)
    relay(3)
    close_group(2)
    close_group(3)
    for g in (side - 2, side - 1):
        for jj in range(side):
            pair_copy(g, jj).wait_send()
    for copy in sent:
        copy.wait_send()


def project_and_scatter(side, call_id, layer, act, weight, residual, bias):
    rows, width = residual.shape
    depth = act.shape[1]
    half = rows // 2
    quad = (side, side, rows, width)
    part = (side, 2, half, width)
    vmem = pl.BlockSpec(memory_space=pltpu.VMEM)
    return pl.pallas_call(
        functools.partial(scatter_kernel, side, layer),
        out_shape=jax.ShapeDtypeStruct((rows, width), jnp.float32),
        in_specs=[vmem, pl.BlockSpec(memory_space=pl.ANY), vmem, vmem],
        out_specs=vmem,
        scratch_shapes=[
            pltpu.VMEM((depth, width), jnp.bfloat16),
            pltpu.VMEM(quad, jnp.bfloat16),
            pltpu.VMEM((2,) + quad[1:], jnp.bfloat16),
            pltpu.VMEM(quad, jnp.bfloat16),
            pltpu.VMEM((side, 4, half, width), jnp.float32),
            pltpu.VMEM(part, jnp.float32),
            pltpu.VMEM((side, 4, half, width), jnp.float32),
            pltpu.VMEM((4, half, width), jnp.float32),
            pltpu.VMEM((2, half, width), jnp.float32),
            pltpu.VMEM((4, half, width), jnp.float32),
            pltpu.SemaphoreType.DMA,
            pltpu.SemaphoreType.DMA((side, side)),
            pltpu.SemaphoreType.DMA((side, side)),
            pltpu.SemaphoreType.DMA((6 * side + 6,)),
            pltpu.SemaphoreType.DMA((6 * side + 6,)),
        ],
        compiler_params=pltpu.CompilerParams(collective_id=call_id, has_side_effects=True, vmem_limit_bytes=VMEM_LIMIT),
        name=f"scatter_{call_id}",
    )(act, weight, residual, bias)


GATHER_ORDER = ((0, 0), (-1, 0), (1, 0), (0, -1), (0, 1), (2, 0), (-1, -1), (-1, 1), (1, -1), (1, 1), (0, 2), (2, -1), (2, 1), (-1, 2), (1, 2), (2, 2))


def gather_kernel(side, layer, gelu, n_out, tail, res_ref, gain_ref, shift_ref, w_hbm, b_ref, *refs):
    tails, refs = (refs[0], refs[1:]) if tail else (None, refs)
    outs, refs = refs[:n_out], refs[n_out:]
    tails_out, refs = (refs[0], refs[1:]) if tail else (None, refs)
    (w_ref, buf, w_sem, send_sem, recv_sem, pair_send, pair_recv) = refs
    load_w = pltpu.make_async_copy(w_hbm.at[layer], w_ref, w_sem)
    load_w.start()
    place = Place(side)
    rows, width = res_ref.shape
    half = rows // 2
    for at in (pl.ds(0, half), pl.ds(half, half)):
        residual = res_ref[at, :]
        centered = residual - jnp.mean(residual, axis=-1, keepdims=True)
        variance = jnp.mean(centered * centered, axis=-1, keepdims=True)
        normed = centered * lax.rsqrt(variance + 1e-5) * gain_ref[layer:layer + 1, :] + shift_ref[layer:layer + 1, :]
        buf[place.me, at, pl.ds(0, width)] = normed.astype(jnp.bfloat16)
    if tail:
        buf[place.me, :, pl.ds(width, tail)] = tails[...]
    place.barrier()

    def view(i, j, h, core=None):
        return buf.at[place.dev(i, j, core), pl.ds(h * half, half)]

    def wrap(k):
        return (k + 1) % side - 1

    def slot(i, j, h):
        return ((i % side) * side + j % side) * 2 + h

    sent = []

    def send(i, j, h, axis, step):
        there = (wrap(i - step), j) if axis == 0 else (i, wrap(j - step))
        device = (place.first, place.second)[axis][step]
        index = slot(i, j, h)
        copy = pltpu.make_async_remote_copy(src_ref=view(i, j, h), dst_ref=view(i, j, h), send_sem=send_sem.at[axis * 2 + (step > 0), index], recv_sem=recv_sem.at[slot(*there, h)], device_id={"tp": device}, device_id_type=MESH)
        copy.start()
        sent.append(copy)

    def pair(i, j, h, core=None):
        index = slot(i, j, h)
        ref = view(i, j, h, core)
        return pltpu.make_async_remote_copy(src_ref=ref, dst_ref=ref, send_sem=pair_send.at[index], recv_sem=pair_recv.at[index], device_id={"tp": place.partner}, device_id_type=MESH)

    def share(i, j, h):
        copy = pair(i, j, h)
        copy.start()
        sent.append(copy)

    def arrived(i, j, h):
        ref = view(i, j, h)
        pltpu.make_async_remote_copy(src_ref=ref, dst_ref=ref, send_sem=send_sem.at[0, 0], recv_sem=recv_sem.at[slot(i, j, h)], device_id={"tp": place.me}, device_id_type=MESH).wait_recv()

    def multiply(shards, core):
        devs = [place.dev(i, j, core) for i, j in shards]
        step = 128 if w_ref.shape[1] % 256 else 256

        def piece(cols, outs, out_cols):
            lhs = jnp.concatenate([buf[d, :, pl.ds(0, width)] for d in devs], axis=0)
            part = jnp.dot(lhs, w_ref[:, cols], preferred_element_type=jnp.float32)
            if gelu:
                part = jax.nn.gelu(part + b_ref[layer:layer + 1, cols], approximate=True)
            part = part.astype(jnp.bfloat16)
            for k, d in enumerate(devs):
                outs[pl.ds(pl.multiple_of(d * rows, rows), rows), out_cols] = part[k * rows:(k + 1) * rows]

        if n_out == 1:
            def body(n, carry):
                cols = pl.ds(pl.multiple_of(n * step, step), step)
                piece(cols, outs[0], cols)
                return carry
            lax.fori_loop(0, w_ref.shape[1] // step, body, 0)
        else:
            if tail:
                for d in devs:
                    tails_out[pl.ds(pl.multiple_of(d * rows, rows), rows), :] = buf[d, :, pl.ds(width, tail)]
            each = w_ref.shape[1] // n_out
            for k in range(n_out):
                piece(pl.ds(k * each, each), outs[k], pl.ds(0, each))

    def forward(i, j, h):
        if j == 0:
            if i == 0:
                send(i, j, h, 0, 1)
                send(i, j, h, 0, -1)
            elif i == -1 and h == 0:
                send(i, j, h, 0, 1)
            elif i == 1 and h == 1:
                send(i, j, h, 0, -1)
            send(i, j, h, 1, 1)
            send(i, j, h, 1, -1)
        elif j == -1 and h == 0:
            send(i, j, h, 1, 1)
        elif j == 1 and h == 1:
            send(i, j, h, 1, -1)
        share(i, j, h)

    for h in range(2):
        forward(0, 0, h)
    load_w.wait()
    count = len(GATHER_ORDER) // 4
    for g in range(count):
        shards = GATHER_ORDER[g * 4:g * 4 + 4]
        lead = [(i, j, 1 if 1 in (i, j) and -1 not in (i, j) else 0) for i, j in shards if (i, j) != (0, 0)]
        for i, j, h in lead + [(i, j, 1 - h) for i, j, h in lead]:
            arrived(i, j, h)
            forward(i, j, h)
        multiply(shards, place.core)
        for i, j in shards:
            for h in range(2):
                pair(i, j, h, 1 - place.core).wait_recv()
        multiply(shards, 1 - place.core)
    for copy in sent:
        copy.wait_send()


def gather_and_project(side, call_id, layer, residual, gain, shift, weight, bias, gelu, n_out, tails=None):
    rows, width = residual.shape
    tail = 0 if tails is None else tails.shape[1]
    extra = [] if tails is None else [tails]
    groups = 2 * side * side
    wide = weight.shape[2]
    vmem = pl.BlockSpec(memory_space=pltpu.VMEM)
    outs = pl.pallas_call(
        functools.partial(gather_kernel, side, layer, gelu, n_out, tail),
        out_shape=[jax.ShapeDtypeStruct((groups * rows, wide // n_out), jnp.bfloat16)] * n_out + [jax.ShapeDtypeStruct((groups * rows, tail), jnp.bfloat16) for _ in extra],
        in_specs=[vmem, vmem, vmem, pl.BlockSpec(memory_space=pl.ANY), vmem] + [vmem for _ in extra],
        out_specs=[vmem] * (n_out + len(extra)),
        scratch_shapes=[
            pltpu.VMEM((width, wide), jnp.bfloat16),
            pltpu.VMEM((groups, rows, width + tail), jnp.bfloat16),
            pltpu.SemaphoreType.DMA,
            pltpu.SemaphoreType.DMA((4, groups)),
            pltpu.SemaphoreType.DMA((groups,)),
            pltpu.SemaphoreType.DMA((groups,)),
            pltpu.SemaphoreType.DMA((groups,)),
        ],
        compiler_params=pltpu.CompilerParams(collective_id=call_id, has_side_effects=True, vmem_limit_bytes=VMEM_LIMIT),
        name=f"gather_{call_id}",
    )(residual, gain, shift, weight, bias, *extra)
    return outs if len(outs) > 1 else outs[0]


def doc_causal_attention(queries, keys_in, values_in, all_ids):
    seq_len = queries.shape[0]
    score_scale = queries.shape[1] ** -0.5
    block_rows = min(QUERY_ROWS, seq_len)
    pieces = []
    for start_row in range(0, seq_len, block_rows):
        stop_row = start_row + block_rows
        scores = jnp.einsum("qe,ke->qk", queries[start_row:stop_row], keys_in[:stop_row], preferred_element_type=jnp.float32) * score_scale
        query_pos = start_row + jnp.arange(block_rows)
        key_pos = jnp.arange(stop_row)
        allowed = (key_pos[None, :] <= query_pos[:, None]) & (all_ids[start_row:stop_row, None] == all_ids[None, :stop_row])
        scores = jnp.where(allowed, scores, -1e30)
        probs_blk = jax.nn.softmax(scores, axis=-1).astype(jnp.bfloat16)
        pieces.append(jnp.einsum("qk,ke->qe", probs_blk, values_in[:stop_row], preferred_element_type=jnp.float32).astype(jnp.bfloat16))
    return jnp.concatenate(pieces, axis=0)


def solution(mesh):
    groups = mesh.shape["tp"]
    side = math.isqrt(groups // 2)
    assert 2 * side * side == groups and side == 4
    row_spec = P("dp", "tp", None)
    vec_spec = P(None, None)
    in_specs = (row_spec, P("dp", "tp"), vec_spec, vec_spec, P(None, None, None, "tp", None), P(None, "tp", None, None), vec_spec, vec_spec, vec_spec, P(None, None, "tp"), P(None, "tp"), P(None, "tp", None), vec_spec)

    def device_fn(tokens, doc_ids, norm1_gain, norm1_shift, qkv_weight, out_weight, out_bias, norm2_gain, norm2_shift, up_weight, up_bias, down_weight, down_bias):
        layers, width = norm1_gain.shape
        id_cols = jnp.broadcast_to(doc_ids[0].astype(jnp.bfloat16)[:, None], (doc_ids.shape[1], 128))
        qkv_flat = qkv_weight.reshape(layers, width, -1)
        residual = tokens[0].astype(jnp.float32)
        for layer in range(layers):
            ids = [4 * layer + k for k in range(4)]
            tails = id_cols if layer == 0 else None
            q, k, v, *gathered = gather_and_project(side, ids[0], layer, residual, norm1_gain, norm1_shift, qkv_flat, norm1_gain, False, 3, tails)
            if layer == 0:
                all_ids = gathered[0][:, 0]
            attn_out = doc_causal_attention(q, k, v, all_ids)
            residual = project_and_scatter(side, ids[1], layer, attn_out, out_weight, residual, out_bias)
            hidden = gather_and_project(side, ids[2], layer, residual, norm2_gain, norm2_shift, up_weight, up_bias, True, 1)
            residual = project_and_scatter(side, ids[3], layer, hidden, down_weight, residual, down_bias)
        return residual.astype(jnp.bfloat16)[None]

    return jax.shard_map(device_fn, mesh=mesh, in_specs=in_specs, out_specs=row_spec, check_vma=False)
```

time: 1320 us -> 721 us (0.55)
  waiting for transfers between devices: 673 us -> 0 us
  Pallas kernels: 0 us -> 665 us
  blocking collectives: 460 us -> 0 us
  matrix products: 110 us -> 14.1 us
  other arithmetic: 32.9 us -> 8.82 us
  local copies, waits for them, and re-layouts: 3.33 us -> 21.2 us
  between operations: 13.9 us -> 0.58 us
    pallas_call x0 -> x8, Pallas kernels: none -> 665 us  [the longest x4 426 us: project_and_scatter(): pl.pallas_call(functools.partial(scatter_kernel, side, layer), out_shape=...]
    all_to_all x2 -> x0, blocking collectives: 408 us -> none  [scatter_sum(): received = lax.all_to_all(split_rows, 'tp', 1, 1, tiled=True)]
    all_to_all x2 -> x0, waiting for transfers between devices: 408 us -> none  [scatter_sum(): received = lax.all_to_all(split_rows, 'tp', 1, 1, tiled=True)]
    all_gather x4 -> x0, waiting for transfers between devices: 265 us -> none  [the longest x2 157 us: device_fn(): full_rows2 = lax.all_gather(normed2, 'tp', axis=1, tiled=True)]
    dot_general x22 -> x16, matrix products: 110 us -> 14.1 us  [the longest x8 8.82 us: doc_causal_attention(): jnp.einsum('qe,ke->qk', queries[start_row:stop_row], keys_in[:stop_row],...]
    unnamed x1 -> x0, blocking collectives: 51.2 us -> none
    reduce_sum x12 -> x0, other arithmetic: 22.6 us -> none  [the longest x4 18.4 us: scatter_sum(): return jnp.sum(received, axis=1, dtype=jnp.float32)]
  transfers between devices with their start and end apart: 6 -> 0, of which waited for: 6 -> 0; matrix products, arithmetic and copies ran while one was open for 0% -> 0% of each run, Pallas kernels for 0% -> 0%
where the time goes in v1:
time: 721 us; the launch traced here: 710 us
  Pallas kernels  665 us (92%)
  local copies, waits for them, and re-layouts  21.2 us (3%)
  matrix products  14.1 us (2%)
  other arithmetic  8.82 us (1%)
    pallas_call x4, Pallas kernels, project_and_scatter(): pl.pallas_call(functools.partial(scatter_kernel, side, layer), out_shape=...  426 us
    pallas_call x4, Pallas kernels, gather_and_project(): pl.pallas_call(functools.partial(gather_kernel, side, layer, gelu, n_out,...  239 us

profile of v1, /device:TPU:97, one launch (start us, length us, event | category | flops | bytes accessed | tf_op | source)
XLA Modules:
  0.0 709.8 jit_solution(15480143058658046674)
XLA Ops:
  0.0 8.7 %copy.15 = bf16[2,4096,3,1,128]{1,4,2,0,3:T(8,128)(2,1)} copy(bf16[2,4096,3,1,128]{4,1,3,2,0:T(8,128)(2,1)} %param.17) | data formatting | bytes 12582912 | tf_op args[4]
  8.7 0.0 copy-start.1
  8.7 0.0 copy-start.8
  8.7 8.7 %copy.16.w_hbm = bf16[2,4096,384]{2,1,0:T(8,128)(2,1)} copy(bf16[2,4096,384]{1,2,0:T(8,128)(2,1)} %bitcast.12) | data formatting | bytes 12582912 | tf_op jit(solution)/shard_map/reshape | solution.py:393
  17.4 0.0 copy-done.1
  17.4 1.1 bitcast_convert_fusion.res_ref
  18.5 0.0 copy-done.8
  18.5 0.7 broadcast_in_dim.22.refs_0_
  19.2 63.1 %gather_0.1 = (bf16[2048,128]{1,0:T(8,128)(2,1)}, bf16[2048,128]{1,0:T(8,128)(2,1)}, bf16[2048,128]{1,0:T(8,128)(2,1)}, bf16[2048,128]{1,0:T(8,128)(2,1)}) custom-call(f32[64,4096]{1,0:T(8,128)} %bitcast_convert_fusion.res_ref, f32[2,4096]{1,0:T(2,128)} %b_ref.6, f32[2,4096]{1,0:T(2,128)} %shift_ref.6, bf16[2,4096,384]{2,1,0:T(8,128)(2,1)} %copy.16.w_hbm, ...), custom_call_target="tpu_custom_call" | custom-call | tf_op jit(solution)/shard_map/gather_0/pallas_call | solution.py:345
  82.3 0.0 copy-start.2
  82.3 1.4 slice_reduce_fusion.6
  83.7 1.3 fusion.47
  85.0 0.0 copy-start
  85.0 0.0 copy-start.3
  85.0 0.0 copy-start.4
  85.0 0.2 fusion.22
  85.2 0.0 copy-done.2
  85.2 0.4 convolution_convert_fusion.1
  85.6 0.4 copy-done
  86.0 0.1 slice_reduce_fusion.2
  86.2 0.0 copy-done.3
  86.2 0.1 copy-done.4
  86.4 0.7 fusion.46
  87.1 0.5 fusion.11
  87.6 0.6 convolution_convert_fusion.3
  88.2 0.2 slice_reduce_fusion.1
  88.4 1.0 fusion.45
  89.4 0.6 fusion.6
  90.0 0.7 fusion.20
  90.7 0.2 slice_reduce_fusion
  90.9 1.3 fusion.44
  92.2 0.7 fusion.1
  93.0 1.1 fusion.18
  94.0 0.8 pad_maximum_fusion.act_ref
  94.9 106.4 %scatter_1.1.res_ref = f32[64,4096]{1,0:T(8,128)} custom-call(bf16[2048,128]{1,0:T(8,128)(2,1)} %pad_maximum_fusion.act_ref, bf16[2,1,128,4096]{3,2,1,0:T(8,128)(2,1)} %w_hbm.9, f32[64,4096]{1,0:T(8,128)} %bitcast_convert_fusion.res_ref, f32[2,4096]{1,0:T(2,128)} %bias_ref.6), custom_call_target="tpu_custom_call" | custom-call | tf_op jit(solution)/shard_map/scatter_1/pallas_call | solution.py:192
  201.3 58.2 %gather_2.1.act_ref = bf16[2048,512]{1,0:T(8,128)(2,1)} custom-call(f32[64,4096]{1,0:T(8,128)} %scatter_1.1.res_ref, f32[2,4096]{1,0:T(2,128)} %gain_ref.7, f32[2,4096]{1,0:T(2,128)} %shift_ref.7, bf16[2,4096,512]{2,1,0:T(8,128)(2,1)} %w_hbm.10, f32[2,512]{1,0:T(2,128)} %b_ref.7), custom_call_target="tpu_custom_call" | custom-call | tf_op jit(solution)/shard_map/gather_2/pallas_call | solution.py:345
  259.5 107.6 %scatter_3.1.res_ref = f32[64,4096]{1,0:T(8,128)} custom-call(bf16[2048,512]{1,0:T(8,128)(2,1)} %gather_2.1.act_ref, bf16[2,512,4096]{2,1,0:T(8,128)(2,1)} %w_hbm.11, f32[64,4096]{1,0:T(8,128)} %scatter_1.1.res_ref, f32[2,4096]{1,0:T(2,128)} %bias_ref.7), custom_call_target="tpu_custom_call" | custom-call | tf_op jit(solution)/shard_map/scatter_3/pallas_call | solution.py:192
  367.2 58.8 %gather_4.1 = (bf16[2048,128]{1,0:T(8,128)(2,1)}, bf16[2048,128]{1,0:T(8,128)(2,1)}, bf16[2048,128]{1,0:T(8,128)(2,1)}) custom-call(f32[64,4096]{1,0:T(8,128)} %scatter_3.1.res_ref, f32[2,4096]{1,0:T(2,128)} %b_ref.6, f32[2,4096]{1,0:T(2,128)} %shift_ref.6, bf16[2,4096,384]{2,1,0:T(8,128)(2,1)} %copy.16.w_hbm, f32[2,4096]{1,0:T(2,128)} %b_ref.6), custom_call_target="tpu_custom_call" | custom-call | tf_op jit(solution)/shard_map/gather_4/pallas_call | solution.py:345
  426.0 0.0 copy-start.5
  426.0 1.4 fusion.51
  427.4 0.0 copy-start.6
  427.4 0.0 copy-start.7
  427.4 0.2 fusion.23
  427.6 0.0 copy-done.5
  427.6 0.4 convolution_convert_fusion
  428.0 0.4 copy-done.6
  428.5 0.2 copy-done.7
  428.6 0.7 fusion.50
  429.4 0.5 fusion.12
  429.9 0.5 convolution_convert_fusion.2
  430.4 1.0 fusion.49
  431.4 0.6 fusion.7
  432.0 0.7 fusion.19
  432.7 1.3 fusion.48
  434.1 0.7 fusion.2
  434.8 0.9 fusion.17
  435.7 0.8 pad_maximum_fusion.1.act_ref
  436.5 105.8 %scatter_5.1.res_ref = f32[64,4096]{1,0:T(8,128)} custom-call(bf16[2048,128]{1,0:T(8,128)(2,1)} %pad_maximum_fusion.1.act_ref, bf16[2,1,128,4096]{3,2,1,0:T(8,128)(2,1)} %w_hbm.9, f32[64,4096]{1,0:T(8,128)} %scatter_3.1.res_ref, f32[2,4096]{1,0:T(2,128)} %bias_ref.6), custom_call_target="tpu_custom_call" | custom-call | tf_op jit(solution)/shard_map/scatter_5/pallas_call | solution.py:192
  542.3 58.4 %gather_6.1.act_ref = bf16[2048,512]{1,0:T(8,128)(2,1)} custom-call(f32[64,4096]{1,0:T(8,128)} %scatter_5.1.res_ref, f32[2,4096]{1,0:T(2,128)} %gain_ref.7, f32[2,4096]{1,0:T(2,128)} %shift_ref.7, bf16[2,4096,512]{2,1,0:T(8,128)(2,1)} %w_hbm.10, f32[2,512]{1,0:T(2,128)} %b_ref.7), custom_call_target="tpu_custom_call" | custom-call | tf_op jit(solution)/shard_map/gather_6/pallas_call | solution.py:345
  600.7 106.6 %scatter_7.1 = f32[64,4096]{1,0:T(8,128)} custom-call(bf16[2048,512]{1,0:T(8,128)(2,1)} %gather_6.1.act_ref, bf16[2,512,4096]{2,1,0:T(8,128)(2,1)} %w_hbm.11, f32[64,4096]{1,0:T(8,128)} %scatter_5.1.res_ref, f32[2,4096]{1,0:T(2,128)} %bias_ref.7), custom_call_target="tpu_custom_call" | custom-call | tf_op jit(solution)/shard_map/scatter_7/pallas_call | solution.py:192
  707.4 2.1 convert_bitcast_fusion
  (4 shorter events, 0.0 us)
Async XLA Ops:
  8.7 8.7 %copy-start.1 = (bf16[1,64,4096]{2,1,0:T(8,128)(2,1)S(1)}, bf16[1,64,4096]{2,1,0:T(8,128)(2,1)}, u32[]{:S(2)}) copy-start(bf16[1,64,4096]{2,1,0:T(8,128)(2,1)} %param.13) | copy-start | bytes 1572868
  8.7 9.8 %copy-start.8 = (s32[1,64]{1,0:T(1,128)S(1)}, s32[1,64]{1,0:T(1,128)}, u32[]{:S(2)}) copy-start(s32[1,64]{1,0:T(1,128)} %param.14) | copy-start | bytes 772
  82.3 2.9 copy-start.2
  85.0 1.0 copy-start
  85.0 1.2 copy-start.3
  85.0 1.3 copy-start.4
  426.0 1.6 copy-start.5
  427.4 1.0 copy-start.6
  427.4 1.2 copy-start.7
